TPU v7x, 256 devices: a whole 4x4x8 slice. The times are simulated.
256 devices in a mesh: member: 16 (over x, y_hi, core), tensor: 16 (over z, y_lo).
Axes of the slice: x: 4, y: 4 (y_hi: 2, y_lo: 2; y = y_hi * 2 + y_lo), z: 8, core: 2. Of those that a mesh axis runs over, the one named last changes fastest.
Arguments:
- prompt_acts: bfloat16 [128, 5120], P(None, 'member'), may hold values from -6 to 6
- gate_weight: bfloat16 [5120, 13824], P('member', 'tensor'), may hold values from -0.078125 to 0.078125
- up_weight: bfloat16 [5120, 13824], P('member', 'tensor'), may hold values from -0.078125 to 0.078125
- down_weight: bfloat16 [13824, 5120], P('tensor', 'member'), may hold values from -0.0546875 to 0.0546875
- d_table: bfloat16 [256, 3, 4, 5120], P('member'), may hold values from -6 to 6
- f_table: bfloat16 [256, 3, 4, 13824], P('member', None, None, 'tensor'), may hold values from -6 to 6
- seeds: int32 [128], P('member'), may hold values from 0 to 15
- fitness: float32 [128], P('member'), may hold values from -6 to 6
Outputs:
- outputs: bfloat16 [128, 128, 5120], P('member', None, 'tensor')
- delta_gate: bfloat16 [5120, 13824], P('member', 'tensor')
- delta_up: bfloat16 [5120, 13824], P('member', 'tensor')
- delta_down: bfloat16 [13824, 5120], P('tensor', 'member')
Inputs may be any that keep to these rules, and one draw needn't show every extreme that they name: Member m uses row (m // 8) * 16 + seeds[m] of both tables, a row in its own group's block.
All inputs are finite; a program needn't handle non-finite values.
Results may differ from a plain program's by a relative error of at most 0.025.
Values may be sent and summed in bfloat16 or wider, within the bound.
A program may use at most 128 MiB of HBM per device.

v0:
```python
import math
import jax
import jax.numpy as jnp
from jax import lax
from jax.sharding import Mesh
from jax.sharding import PartitionSpec as P

D = 5120
FFW = 13824
MEMBER = ("member_0", "member_1", "member_2")
TENSOR = ("tensor_0", "tensor_1")
perturb_gain = 0.5


def sent_to_all(shard, axis):
    devices = lax.axis_size(axis)
    return lax.all_to_all(
        jnp.broadcast_to(shard[None], (devices, *shard.shape)), axis, 0, 0, tiled=True
    )


def joined_along(parts, dim):
    dims = list(parts.shape[1:])
    dims[dim] *= parts.shape[0]
    return jnp.moveaxis(parts, 0, dim).reshape(dims)


def gather_axes(shard, axes, dim):
    far, near = axes
    leading = sent_to_all(shard, far)
    parts = jnp.swapaxes(sent_to_all(leading, near), 0, 1)
    return joined_along(parts.reshape(-1, *shard.shape), dim)


def gather_directly(shard, axis, dim):
    return joined_along(sent_to_all(shard, axis), dim)


def filled_up(lines, devices):
    spare = -len(lines) % devices
    return jnp.pad(lines, [(0, spare)] + [(0, 0)] * (lines.ndim - 1))


def cut_along(shard, dim, devices):
    before, after = (shard.shape[:dim], shard.shape[dim + 1 :])
    return jnp.moveaxis(shard.reshape(*before, devices, -1, *after), dim, 0)


def sent_and_summed(shard, axis, dim):
    devices = lax.axis_size(axis)
    parts = lax.all_to_all(cut_along(shard, dim, devices), axis, 0, 0, tiled=True)
    return jnp.sum(parts.astype(jnp.float32), axis=0)


def sum_in_two_steps(shard, axes, dim):
    far, near = axes
    own = sent_and_summed(cut_along(shard, dim, lax.axis_size(far)), near, dim + 1)
    return jnp.sum(
        lax.all_to_all(own.astype(jnp.bfloat16), far, 0, 0, tiled=True).astype(jnp.float32), axis=0
    )


def sum_by_parts(shard, axes):
    lines = shard.reshape(-1, shard.shape[-1])
    padded = filled_up(lines, lax.axis_size(axes[0]) * lax.axis_size(axes[1]))
    whole = gather_axes(sum_in_two_steps(padded, axes, 0).astype(jnp.bfloat16), axes, 0)
    return lax.slice_in_dim(whole, 0, len(lines)).reshape(shard.shape).astype(jnp.float32)


def taken_together(shard, axis):
    return sent_to_all(shard, axis).sum(axis=0)


def scatter_axes(shard, axes, dim):
    if not axes:
        return shard
    nearer = lax.psum_scatter(shard, axes[0], scatter_dimension=dim, tiled=True)
    return scatter_axes(nearer, axes[1:], dim)


def shards(prompt_acts, gate_weight, up_weight, down_weight, d_table, f_table, seeds, fitness):
    members = seeds.shape[0]
    prompt_len = prompt_acts.shape[0]
    rank_size = d_table.shape[2]
    d_sel = jnp.take(d_table, seeds, axis=0)
    selected_factors = jnp.take(f_table, seeds, axis=0)
    d_slices = lax.all_to_all(d_sel, MEMBER, split_axis=3, concat_axis=0, tiled=True)
    f_all, fit_all = (
        gather_axes(selected_factors, (("member_0", "member_1"), "member_2"), 0),
        gather_axes(fitness.astype(jnp.bfloat16), (("member_0", "member_1"), "member_2"), 0).astype(
            fitness.dtype
        ),
    )
    population = fit_all.shape[0]
    gate_part = jnp.dot(prompt_acts, gate_weight, preferred_element_type=jnp.float32)
    up_part = jnp.dot(prompt_acts, up_weight, preferred_element_type=jnp.float32)
    prompt_full = gather_directly(prompt_acts, MEMBER, 1)
    gate_sum, up_sum = (
        sum_by_parts(gate_part.astype(jnp.bfloat16), (("member_0", "member_1"), "member_2")),
        sum_by_parts(up_part.astype(jnp.bfloat16), (("member_0", "member_1"), "member_2")),
    )
    in_factors = d_sel[:, :2].reshape(members * 2 * rank_size, D)
    proj_sum = jnp.dot(prompt_full, in_factors.T, preferred_element_type=jnp.float32)
    base_gate = gate_sum.astype(jnp.bfloat16)
    base_up = up_sum.astype(jnp.bfloat16)
    proj_inputs = (
        (proj_sum / math.sqrt(D)).astype(jnp.bfloat16).reshape(prompt_len, members, 2, rank_size)
    )
    perturbed = jnp.einsum(
        "pmkr,mkrf->mkpf", proj_inputs, selected_factors[:, :2], preferred_element_type=jnp.float32
    )
    gate = base_gate.astype(jnp.float32)[None] + perturb_gain * perturbed[:, 0]
    up = base_up.astype(jnp.float32)[None] + perturb_gain * perturbed[:, 1]
    hidden_state = (jax.nn.silu(gate) * up).astype(jnp.bfloat16)
    projection_here = jnp.einsum(
        "cdv,czv->cdz", hidden_state, selected_factors[:, 2], preferred_element_type=jnp.float32
    )
    proj_down = (taken_together(projection_here, TENSOR) / math.sqrt(FFW)).astype(jnp.bfloat16)
    hidden_rows = hidden_state.reshape(members * prompt_len, hidden_state.shape[2])
    partial_value = jnp.dot(
        hidden_rows,
        lax.all_gather(down_weight, MEMBER, axis=1, tiled=True),
        preferred_element_type=jnp.float32,
    )
    summed = scatter_axes(partial_value.astype(jnp.bfloat16), TENSOR, 1).astype(jnp.float32)
    local_column_range = summed.shape[1]
    col_start = lax.axis_index(TENSOR) * local_column_range
    out_factor = lax.dynamic_slice_in_dim(d_sel[:, 2], col_start, local_column_range, 2)
    down_noise_delta = perturb_gain * jnp.einsum(
        "mpr,mrd->mpd", proj_down, out_factor, preferred_element_type=jnp.float32
    )
    outputs = (summed.reshape(members, prompt_len, local_column_range) + down_noise_delta).astype(
        jnp.bfloat16
    )
    mean = jnp.sum(fit_all) / population
    spread = jnp.sum((fit_all - mean) ** 2) / population
    score = (fit_all - mean) / jnp.sqrt(spread + 1.0)
    weighted = (d_slices.astype(jnp.float32) * score[:, None, None, None]).astype(jnp.bfloat16)
    scale = 1.0 / math.sqrt(population * rank_size)
    width_cols = weighted.shape[3]
    hidden_cols = f_all.shape[3]
    w_gate = weighted[:, 0].reshape(population * rank_size, width_cols)
    w_up = weighted[:, 1].reshape(population * rank_size, width_cols)
    w_down = weighted[:, 2].reshape(population * rank_size, width_cols)
    f_gate = f_all[:, 0].reshape(population * rank_size, hidden_cols)
    f_up = f_all[:, 1].reshape(population * rank_size, hidden_cols)
    down_factor_columns = f_all[:, 2].reshape(population * rank_size, hidden_cols)
    delta_gate = (jnp.dot(w_gate.T, f_gate, preferred_element_type=jnp.float32) * scale).astype(
        jnp.bfloat16
    )
    delta_up = (jnp.dot(w_up.T, f_up, preferred_element_type=jnp.float32) * scale).astype(
        jnp.bfloat16
    )
    delta_down = (
        jnp.dot(down_factor_columns.T, w_down, preferred_element_type=jnp.float32) * scale
    ).astype(jnp.bfloat16)
    return (outputs, delta_gate, delta_up, delta_down)


def solution(mesh):
    split = Mesh(
        mesh.devices.reshape(4, 2, 2, 8, 2),
        ("member_0", "member_1", "member_2", "tensor_0", "tensor_1"),
    )
    placed = (
        P(None, MEMBER),
        P(MEMBER, TENSOR),
        P(MEMBER, TENSOR),
        P(TENSOR, MEMBER),
        P(MEMBER, None, None, None),
        P(MEMBER, None, None, TENSOR),
        P(MEMBER),
        P(MEMBER),
    )
    return jax.shard_map(
        shards,
        mesh=split,
        in_specs=placed,
        out_specs=(
            P(MEMBER, None, TENSOR),
            P(MEMBER, TENSOR),
            P(MEMBER, TENSOR),
            P(TENSOR, MEMBER),
        ),
        check_vma=False,
    )
```

profile of v0, /device:TPU:2, one launch (start us, length us, event | category | flops | bytes accessed | tf_op | source)
XLA Modules:
  0.0 367.8 jit_solution(5300602378496376444)
XLA Ops:
  7.2 0.7 all-gather.2.cloned.1.call-update
  7.9 1.5 convolution_convert_fusion.1
  9.6 0.7 copy.151
  10.3 3.4 all-to-all-start.5
  13.8 1.5 convolution_convert_fusion.2
  15.5 0.7 copy.144
  16.2 3.4 all-to-all-start
  19.6 0.7 reduce_sum.77
  20.3 0.8 all-to-all-done
  21.2 7.5 %all-to-all-start.6 = ((bf16[8,8,864]{2,1,0:T(8,128)(2,1)}), bf16[8,8,864]{2,1,0:T(8,128)(2,1)S(1)}, u32[]{:S(2)}, u32[]{:S(2)}) async-start(bf16[8,8,864]{2,1,0:T(8,128)(2,1)} %reduce_sum.77), calls=%async_computation.6 | async-start | bytes 229376 | tf_op jit(solution)/shard_map/all_to_all | solution.py:59
  28.6 0.7 reduce_sum.75
  29.3 6.2 %all-to-all-done.6 = bf16[8,8,864]{2,1,0:T(8,128)(2,1)S(1)} async-done(((bf16[8,8,864]{2,1,0:T(8,128)(2,1)}), bf16[8,8,864]{2,1,0:T(8,128)(2,1)S(1)}, u32[]{:S(2)}, u32[]{:S(2)}) %all-to-all-start.6) | async-done | bytes 110624 | tf_op jit(solution)/shard_map/all_to_all | solution.py:59
  35.5 5.4 %all-to-all-start.1 = ((bf16[8,8,864]{2,1,0:T(8,128)(2,1)}), bf16[8,8,864]{2,1,0:T(8,128)(2,1)S(1)}, u32[]{:S(2)}, u32[]{:S(2)}) async-start(bf16[8,8,864]{2,1,0:T(8,128)(2,1)} %reduce_sum.75), calls=%async_computation.1 | async-start | bytes 229376 | tf_op jit(solution)/shard_map/all_to_all | solution.py:59
  40.9 6.3 %all-to-all-done.1 = bf16[8,8,864]{2,1,0:T(8,128)(2,1)S(1)} async-done(((bf16[8,8,864]{2,1,0:T(8,128)(2,1)}), bf16[8,8,864]{2,1,0:T(8,128)(2,1)S(1)}, u32[]{:S(2)}, u32[]{:S(2)}) %all-to-all-start.1) | async-done | bytes 110624 | tf_op jit(solution)/shard_map/all_to_all | solution.py:59
  47.2 0.7 broadcast_in_dim.52
  47.9 4.8 %all-to-all-start.7 = ((bf16[8,8,864]{2,1,0:T(8,128)(2,1)}), bf16[8,8,864]{2,1,0:T(8,128)(2,1)S(1)}, u32[]{:S(2)}, u32[]{:S(2)}) async-start(bf16[8,8,864]{2,1,0:T(8,128)(2,1)} %broadcast_in_dim.52), calls=%async_computation.7 | async-start | bytes 229376 | tf_op jit(solution)/shard_map/all_to_all | solution.py:17
  52.7 6.4 %all-to-all-done.7 = bf16[8,8,864]{2,1,0:T(8,128)(2,1)S(1)} async-done(((bf16[8,8,864]{2,1,0:T(8,128)(2,1)}), bf16[8,8,864]{2,1,0:T(8,128)(2,1)S(1)}, u32[]{:S(2)}, u32[]{:S(2)}) %all-to-all-start.7) | async-done | bytes 110624 | tf_op jit(solution)/shard_map/all_to_all | solution.py:17
  59.1 3.9 %all_to_all.80 = bf16[2,8,8,864]{3,2,1,0:T(8,128)(2,1)S(1)} all-to-all(bf16[2,8,8,864]{3,2,1,0:T(8,128)(2,1)S(1)} %broadcast_in_dim.53), channel_id=1, replica_groups=mesh['member_0'=4,'member_1'=2,'member_2'=2,'tensor_0'=8,'tensor_1'=2] {..., dimensions={0} | all-to-all | bytes 442368 | tf_op jit(solution)/shard_map/all_to_all | solution.py:17
  63.0 0.7 broadcast_in_dim.44
  63.6 4.9 %all-to-all-start.2 = ((bf16[8,8,864]{2,1,0:T(8,128)(2,1)}), bf16[8,8,864]{2,1,0:T(8,128)(2,1)S(1)}, u32[]{:S(2)}, u32[]{:S(2)}) async-start(bf16[8,8,864]{2,1,0:T(8,128)(2,1)} %broadcast_in_dim.44), calls=%async_computation.2 | async-start | bytes 229376 | tf_op jit(solution)/shard_map/all_to_all | solution.py:17
  68.5 2.3 gather_fusion
  70.8 4.4 %all-to-all-done.2 = bf16[8,8,864]{2,1,0:T(8,128)(2,1)S(1)} async-done(((bf16[8,8,864]{2,1,0:T(8,128)(2,1)}), bf16[8,8,864]{2,1,0:T(8,128)(2,1)S(1)}, u32[]{:S(2)}, u32[]{:S(2)}) %all-to-all-start.2) | async-done | bytes 110624 | tf_op jit(solution)/shard_map/all_to_all | solution.py:17
  75.2 4.6 %all_to_all.81 = bf16[2,8,8,864]{3,2,1,0:T(8,128)(2,1)} all-to-all(bf16[2,8,8,864]{3,2,1,0:T(8,128)(2,1)S(1)} %broadcast_in_dim.45), channel_id=1, replica_groups=mesh['member_0'=4,'member_1'=2,'member_2'=2,'tensor_0'=8,'tensor_1'=2] {..., dimensions={0} | all-to-all | bytes 442368 | tf_op jit(solution)/shard_map/all_to_all | solution.py:17
  79.8 1.3 broadcast_in_dim.49
  81.1 5.3 %all-to-all-start.4 = ((bf16[16,128,320]{1,2,0:T(8,128)(2,1)}), bf16[16,128,320]{1,2,0:T(8,128)(2,1)S(1)}, u32[]{:S(2)}, u32[]{:S(2)}) async-start(bf16[16,128,320]{1,2,0:T(8,128)(2,1)} %broadcast_in_dim.49), calls=%async_computation.4 | async-start | bytes 2621440 | tf_op jit(solution)/shard_map/all_to_all | solution.py:17
  86.7 1.7 broadcast_select_fusion
  88.4 0.7 gather_fusion.1
  89.1 1.1 slice.52
  90.2 1.5 reshape.108
  91.7 0.8 broadcast_select_fusion.1
  92.6 1.0 copy.181
  93.5 1.0 convert_bitcast_fusion.2
  94.5 1.0 copy.180
  95.5 12.5 %all-to-all-done.4 = bf16[16,128,320]{1,2,0:T(8,128)(2,1)S(1)} async-done(((bf16[16,128,320]{1,2,0:T(8,128)(2,1)}), bf16[16,128,320]{1,2,0:T(8,128)(2,1)S(1)}, u32[]{:S(2)}, u32[]{:S(2)}) %all-to-all-start.4) | async-done | bytes 1310752 | tf_op jit(solution)/shard_map/all_to_all | solution.py:17
  108.4 2.1 fusion.18
  110.8 3.8 %copy.156 = f32[8,1,128,864]{2,0,3,1:T(8,128)} copy(f32[8,1,128,864]{2,3,1,0:T(8,128)S(1)} %slice_multiply_fusion) | data formatting | bytes 7077888 | tf_op jit(solution)/shard_map/mul | solution.py:113
  114.9 3.8 %copy.149 = f32[8,1,128,864]{2,0,3,1:T(8,128)} copy(f32[8,1,128,864]{2,3,0,1:T(8,128)S(1)} %fusion.2) | data formatting | bytes 7077888 | tf_op jit(solution)/shard_map/mul | solution.py:112
  118.7 2.1 add.60.clone
  120.8 2.0 add.55.clone
  122.8 25.7 %convolution_convert_fusion = bf16[1024,5120]{1,0:T(8,128)(2,1)} fusion(bf16[864,5120]{0,1:T(8,128)(2,1)} %all-gather.2.cloned.1.call-done, f32[108,8,8,128]{3,2,1,0:T(8,128)} %bitcast.163, f32[108,8,8,128]{3,2,1,0:T(8,128)} %bitcast.165, f32[108,8,8,128]{3,2,1,0:T(8,128)} %bitcast.164, f32[108,8,8,128]{3,2,1,0:T(8,128)} %bitcast.166), kind=kOutput, calls=%fused_computation.2 | convolution fusion | flops 9072017408 | bytes 33488896 | tf_op jit(solution)/shard_map/dot_general | solution.py:120
  148.5 14.4 %copy.171 = bf16[1024,5120]{0,1:T(8,128)(2,1)} copy(bf16[1024,5120]{1,0:T(8,128)(2,1)} %convolution_convert_fusion) | data formatting | bytes 20971520
  164.1 8.8 %all-to-all-start.11 = ((bf16[8,1,8]{2,1,0:T(2,128)(2,1)}), bf16[8,1,8]{2,1,0:T(2,128)(2,1)S(1)}, u32[]{:S(2)}, u32[]{:S(2)}) async-start(bf16[8,1,8]{2,1,0:T(2,128)(2,1)} %broadcast_in_dim.98), calls=%async_computation.11 | async-start | bytes 8192 | tf_op jit(solution)/shard_map/all_to_all | solution.py:17
  172.9 15.0 %copy.161 = bf16[8,3,4,5120]{0,2,1,3:T(4,128)(2,1)} copy(bf16[8,3,4,5120]{3,2,1,0:T(4,128)(2,1)S(1)} %broadcast_select_fusion) | data formatting | bytes 1966080 | tf_op jit(solution)/shard_map/jit(_take)/select_n | solution.py:85
  188.0 20.0 %reshape.151 = bf16[16,2,15360]{2,1,0:T(2,128)(2,1)} reshape(bf16[5120,3,4,8]{3,2,1,0:T(4,128)(2,1)} %bitcast.156) | data formatting | bytes 1966080
  208.0 3.7 %all_to_all.82 = bf16[2,8,8]{2,1,0:T(8,128)(2,1)S(1)} all-to-all(bf16[2,8,8]{2,1,0:T(8,128)(2,1)S(1)} %broadcast_in_dim.100), channel_id=1, replica_groups=mesh['member_0'=4,'member_1'=2,'member_2'=2,'tensor_0'=8,'tensor_1'=2] {..., dimensions={0} | all-to-all | bytes 512 | tf_op jit(solution)/shard_map/all_to_all | solution.py:17
  211.7 7.2 %all-to-all-start.10 = ((bf16[16,2,15360]{2,1,0:T(2,128)(2,1)}), bf16[16,2,15360]{2,1,0:T(2,128)(2,1)S(1)}, u32[]{:S(2)}, u32[]{:S(2)}) async-start(bf16[16,2,15360]{2,1,0:T(2,128)(2,1)} %reshape.151), calls=%async_computation.10 | async-start | bytes 1966080 | tf_op jit(solution)/shard_map/all_to_all | solution.py:87
  218.9 15.0 %all-to-all-done.10 = bf16[16,2,15360]{2,1,0:T(2,128)(2,1)S(1)} async-done(((bf16[16,2,15360]{2,1,0:T(2,128)(2,1)}), bf16[16,2,15360]{2,1,0:T(2,128)(2,1)S(1)}, u32[]{:S(2)}, u32[]{:S(2)}) %all-to-all-start.10) | async-done | bytes 983072 | tf_op jit(solution)/shard_map/all_to_all | solution.py:87
  234.0 1.2 broadcast_in_dim.101
  235.2 6.4 %all-to-all-start.13 = ((bf16[8,8,3,4,864]{4,1,3,2,0:T(8,128)(2,1)}), bf16[8,8,3,4,864]{4,1,3,2,0:T(8,128)(2,1)}, u32[]{:S(2)}, u32[]{:S(2)}) async-start(bf16[8,8,3,4,864]{4,1,3,2,0:T(8,128)(2,1)} %broadcast_in_dim.101), calls=%async_computation.13 | async-start | bytes 2752512 | tf_op jit(solution)/shard_map/all_to_all | solution.py:17
  241.6 39.1 %reduce-scatter.7.cloned.1.call-done = bf16[640,1024]{1,0:T(8,128)(2,1)} async-done(((bf16[5120,1024]{1,0:T(8,128)(2,1)}), bf16[640,1024]{1,0:T(8,128)(2,1)}) %reduce-scatter.7.cloned.1.call-update) | async-done | bytes 1310736
  283.5 19.3 %reshape.152 = bf16[5120,3,4,8]{3,2,1,0:T(4,128)(2,1)} reshape(bf16[16,2,15360]{2,1,0:T(2,128)(2,1)S(1)} %all-to-all-done.10) | data formatting | bytes 1966080
  302.8 21.0 %copy.162 = f32[8,3,4,16,320]{4,0,3,2,1:T(8,128)} copy(bf16[8,3,4,16,320]{0,2,1,4,3:T(4,128)(2,1)} %bitcast.155) | data formatting | bytes 2949120 | tf_op jit(solution)/shard_map/convert_element_type | solution.py:138
  323.8 2.0 copy.164
  326.1 1.9 copy.166
  328.4 6.2 %all_to_all.83 = bf16[2,8,8,3,4,864]{5,2,1,4,3,0:T(8,128)(2,1)S(1)} all-to-all(bf16[2,8,8,3,4,864]{5,2,1,4,3,0:T(8,128)(2,1)S(1)} %broadcast_in_dim.102), channel_id=1, replica_groups=mesh['member_0'=4,'member_1'=2,'member_2'=2,'tensor_0'=8,'tensor_1'=2] {..., dimensions={0} | all-to-all | bytes 5308416 | tf_op jit(solution)/shard_map/all_to_all | solution.py:17
  334.9 1.3 fusion.16
  336.2 1.4 slice-done.1
  337.7 2.3 fusion.7
  340.0 0.7 broadcast_in_dim.54
  340.7 5.5 %all-to-all-start.9 = ((f32[16,8,128,4]{2,1,3,0:T(8,128)}), f32[16,8,128,4]{2,1,3,0:T(8,128)S(1)}, u32[]{:S(2)}, u32[]{:S(2)}) async-start(f32[16,8,128,4]{2,1,3,0:T(8,128)} %broadcast_in_dim.54), calls=%async_computation.9 | async-start | bytes 524288 | tf_op jit(solution)/shard_map/all_to_all | solution.py:17
  346.3 2.6 fusion.15
  348.9 2.6 fusion.14
  351.5 7.2 %all-to-all-done.9 = f32[16,8,128,4]{2,1,3,0:T(8,128)S(1)} async-done(((f32[16,8,128,4]{2,1,3,0:T(8,128)}), f32[16,8,128,4]{2,1,3,0:T(8,128)S(1)}, u32[]{:S(2)}, u32[]{:S(2)}) %all-to-all-start.9) | async-done | bytes 262176 | tf_op jit(solution)/shard_map/all_to_all | solution.py:17
  358.8 2.5 fusion.13
  (75 shorter events, 5.3 us)
Async XLA Ops:
  7.2 61.3 %copy-start = (bf16[16,3,4,5120]{3,2,1,0:T(4,128)(2,1)S(1)}, bf16[16,3,4,5120]{3,2,1,0:T(4,128)(2,1)}, u32[]{:S(2)}) copy-start(bf16[16,3,4,5120]{3,2,1,0:T(4,128)(2,1)} %param.12) | copy-start | bytes 5898244
  7.2 33.7 %copy-start.12 = (s32[8]{0:T(128)S(1)}, s32[8]{0:T(128)}, u32[]{:S(2)}) copy-start(s32[8]{0:T(128)} %param.14) | copy-start | bytes 100
  7.2 111.5 %all-gather.2.cloned.1.call-start = ((), (), s32[]{:S(2)}) async-start(), calls=%async_computation.17 | async-start | bytes 9748480 | tf_op jit(solution)/shard_map/all_gather | solution.py:122
  10.3 5.9 %all-to-all-start.5 = ((bf16[2,8,8,864]{3,2,1,0:T(8,128)(2,1)}), bf16[2,8,8,864]{3,2,1,0:T(8,128)(2,1)S(1)}, u32[]{:S(2)}, u32[]{:S(2)}) async-start(bf16[2,8,8,864]{3,2,1,0:T(8,128)(2,1)} %copy.151), calls=%async_computation.5 | async-start | bytes 458752 | tf_op jit(solution)/shard_map/all_to_all | solution.py:51
  15.3 64.5 %copy-start.10 = (bf16[128,320]{0,1:T(8,128)(2,1)S(1)}, bf16[128,320]{0,1:T(8,128)(2,1)}, u32[]{:S(2)}) copy-start(bf16[128,320]{0,1:T(8,128)(2,1)} %param.8) | copy-start | bytes 245764
  16.2 5.0 %all-to-all-start = ((bf16[2,8,8,864]{3,2,1,0:T(8,128)(2,1)}), bf16[2,8,8,864]{3,2,1,0:T(8,128)(2,1)S(1)}, u32[]{:S(2)}, u32[]{:S(2)}) async-start(bf16[2,8,8,864]{3,2,1,0:T(8,128)(2,1)} %copy.144), calls=%async_computation | async-start | bytes 458752 | tf_op jit(solution)/shard_map/all_to_all | solution.py:51
  21.2 14.3 %all-to-all-start.6 = ((bf16[8,8,864]{2,1,0:T(8,128)(2,1)}), bf16[8,8,864]{2,1,0:T(8,128)(2,1)S(1)}, u32[]{:S(2)}, u32[]{:S(2)}) async-start(bf16[8,8,864]{2,1,0:T(8,128)(2,1)} %reduce_sum.77), calls=%async_computation.6 | async-start | bytes 229376 | tf_op jit(solution)/shard_map/all_to_all | solution.py:59
  35.5 11.7 %all-to-all-start.1 = ((bf16[8,8,864]{2,1,0:T(8,128)(2,1)}), bf16[8,8,864]{2,1,0:T(8,128)(2,1)S(1)}, u32[]{:S(2)}, u32[]{:S(2)}) async-start(bf16[8,8,864]{2,1,0:T(8,128)(2,1)} %reduce_sum.75), calls=%async_computation.1 | async-start | bytes 229376 | tf_op jit(solution)/shard_map/all_to_all | solution.py:59
  47.9 11.2 %all-to-all-start.7 = ((bf16[8,8,864]{2,1,0:T(8,128)(2,1)}), bf16[8,8,864]{2,1,0:T(8,128)(2,1)S(1)}, u32[]{:S(2)}, u32[]{:S(2)}) async-start(bf16[8,8,864]{2,1,0:T(8,128)(2,1)} %broadcast_in_dim.52), calls=%async_computation.7 | async-start | bytes 229376 | tf_op jit(solution)/shard_map/all_to_all | solution.py:17
  63.6 11.6 %all-to-all-start.2 = ((bf16[8,8,864]{2,1,0:T(8,128)(2,1)}), bf16[8,8,864]{2,1,0:T(8,128)(2,1)S(1)}, u32[]{:S(2)}, u32[]{:S(2)}) async-start(bf16[8,8,864]{2,1,0:T(8,128)(2,1)} %broadcast_in_dim.44), calls=%async_computation.2 | async-start | bytes 229376 | tf_op jit(solution)/shard_map/all_to_all | solution.py:17
  70.8 17.6 %copy-start.11 = (bf16[16,3,4,864]{3,2,1,0:T(4,128)(2,1)S(1)}, bf16[16,3,4,864]{3,2,1,0:T(4,128)(2,1)}, u32[]{:S(2)}) copy-start(bf16[16,3,4,864]{3,2,1,0:T(4,128)(2,1)} %param.13) | copy-start | bytes 995332
  81.1 26.9 %all-to-all-start.4 = ((bf16[16,128,320]{1,2,0:T(8,128)(2,1)}), bf16[16,128,320]{1,2,0:T(8,128)(2,1)S(1)}, u32[]{:S(2)}, u32[]{:S(2)}) async-start(bf16[16,128,320]{1,2,0:T(8,128)(2,1)} %broadcast_in_dim.49), calls=%async_computation.4 | async-start | bytes 2621440 | tf_op jit(solution)/shard_map/all_to_all | solution.py:17
  86.4 194.3 %reduce-scatter.7.cloned.1.call-start = ((), (), s32[]{:S(2)}) async-start(), calls=%async_computation.18 | async-start | bytes 11796480
  88.4 192.4 %copy-start.3 = (bf16[8,3,4,5120]{3,2,1,0:T(4,128)(2,1)}, bf16[8,3,4,5120]{3,2,1,0:T(4,128)(2,1)S(1)}, u32[]{:S(2)}) copy-start(bf16[8,3,4,5120]{3,2,1,0:T(4,128)(2,1)S(1)} %broadcast_select_fusion) | copy-start | bytes 2949124
  110.5 4.1 %copy-start.2 = (f32[8,2,128,864]{2,3,1,0:T(8,128)}, f32[8,2,128,864]{2,3,1,0:T(8,128)S(1)}, u32[]{:S(2)}) copy-start(f32[8,2,128,864]{2,3,1,0:T(8,128)S(1)} %fusion.18) | copy-start | bytes 21233668
  114.9 3.8 %copy-start.5 = (f32[128,864]{0,1:T(8,128)S(1)}, f32[128,864]{0,1:T(8,128)}, u32[]{:S(2)}) copy-start(f32[128,864]{0,1:T(8,128)} %copy.181) | copy-start | bytes 1327108
  118.7 2.1 copy-start.6
  162.9 0.7 copy-start.13
  164.1 43.8 %all-to-all-start.11 = ((bf16[8,1,8]{2,1,0:T(2,128)(2,1)}), bf16[8,1,8]{2,1,0:T(2,128)(2,1)S(1)}, u32[]{:S(2)}, u32[]{:S(2)}) async-start(bf16[8,1,8]{2,1,0:T(2,128)(2,1)} %broadcast_in_dim.98), calls=%async_computation.11 | async-start | bytes 8192 | tf_op jit(solution)/shard_map/all_to_all | solution.py:17
  188.0 30.9 %copy-start.8 = (bf16[8,3,4,864]{3,2,1,0:T(4,128)(2,1)S(1)}, bf16[8,3,4,864]{3,2,1,0:T(4,128)(2,1)}, u32[]{:S(2)}) copy-start(bf16[8,3,4,864]{3,2,1,0:T(4,128)(2,1)} %broadcast_select_fusion.1) | copy-start | bytes 497668
  211.7 22.3 %all-to-all-start.10 = ((bf16[16,2,15360]{2,1,0:T(2,128)(2,1)}), bf16[16,2,15360]{2,1,0:T(2,128)(2,1)S(1)}, u32[]{:S(2)}, u32[]{:S(2)}) async-start(bf16[16,2,15360]{2,1,0:T(2,128)(2,1)} %reshape.151), calls=%async_computation.10 | async-start | bytes 1966080 | tf_op jit(solution)/shard_map/all_to_all | solution.py:87
  235.2 90.9 %all-to-all-start.13 = ((bf16[8,8,3,4,864]{4,1,3,2,0:T(8,128)(2,1)}), bf16[8,8,3,4,864]{4,1,3,2,0:T(8,128)(2,1)}, u32[]{:S(2)}, u32[]{:S(2)}) async-start(bf16[8,8,3,4,864]{4,1,3,2,0:T(8,128)(2,1)} %broadcast_in_dim.101), calls=%async_computation.13 | async-start | bytes 2752512 | tf_op jit(solution)/shard_map/all_to_all | solution.py:17
  241.6 117.1 %reduce-scatter.9.cloned.1.call-start = ((), (), s32[]{:S(2)}) async-start(), calls=%async_computation.19 | async-start | bytes 1966080
  326.0 8.8 %copy-start.9 = (bf16[128,3,4,320]{0,3,2,1:T(8,128)(2,1)}, bf16[128,3,4,320]{0,3,2,1:T(8,128)(2,1)S(1)}, u32[]{:S(2)}) copy-start(bf16[128,3,4,320]{0,3,2,1:T(8,128)(2,1)S(1)} %multiply_convert_fusion) | copy-start | bytes 2949124
  328.4 7.8 %slice-start = ((s8[7077888]{0:T(1024)(128)(4,1)}), s8[4194304]{0:T(1024)(128)(4,1)S(1)}, s32[]{:S(2)}) async-start(s8[7077888]{0:T(1024)(128)(4,1)} %bitcast.158), calls=%async_computation.20 | async-start | bytes 8388608
  334.6 3.0 slice-start.1
  334.6 3.1 copy-start.7
  334.8 5.1 %copy-start.4 = (bf16[8,2,8,3,4,864]{5,2,1,0,4,3:T(8,128)(2,1)}, bf16[8,2,8,3,4,864]{5,2,1,0,4,3:T(8,128)(2,1)S(1)}, u32[]{:S(2)}) copy-start(bf16[8,2,8,3,4,864]{5,2,1,0,4,3:T(8,128)(2,1)S(1)} %copy.167) | copy-start | bytes 7962628
  340.0 18.8 %slice-start.2 = ((bf16[8,3,4,5120]{3,2,1,0:T(4,128)(2,1)}), bf16[8,1,4,5120]{3,2,1,0:T(4,128)(2,1)S(1)}, s32[]{:S(2)}) async-start(bf16[8,3,4,5120]{3,2,1,0:T(4,128)(2,1)} %copy-done.3), calls=%async_computation.22 | async-start | bytes 655360 | tf_op jit(solution)/shard_map/slice | solution.py:128
  340.0 21.3 %copy-start.1 = (bf16[16,3,4,5120]{3,2,1,0:T(4,128)(2,1)S(1)}, bf16[16,3,4,5120]{3,2,1,0:T(4,128)(2,1)}, u32[]{:S(2)}) copy-start(bf16[16,3,4,5120]{3,2,1,0:T(4,128)(2,1)} %param.12) | copy-start | bytes 5898244
  340.7 17.9 %all-to-all-start.9 = ((f32[16,8,128,4]{2,1,3,0:T(8,128)}), f32[16,8,128,4]{2,1,3,0:T(8,128)S(1)}, u32[]{:S(2)}, u32[]{:S(2)}) async-start(f32[16,8,128,4]{2,1,3,0:T(8,128)} %broadcast_in_dim.54), calls=%async_computation.9 | async-start | bytes 524288 | tf_op jit(solution)/shard_map/all_to_all | solution.py:17
Sparse Core Ops, SparseCore 0:
  10.7 98.1 all-gather.1
  163.0 117.7 reduce-scatter.6
  283.3 26.9 reduce-scatter.8
where the time goes:
time: 371 us; the launch traced here: 368 us
  local copies, waits for them, and re-layouts  123 us (33%)
  waiting for transfers between devices  98.7 us (27%)
  starting transfers between devices  62.9 us (17%)
  matrix products  42.5 us (11%)
  blocking collectives  18.4 us (5%)
  between operations  15.5 us (4%)
  other arithmetic  6.97 us (2%)
    unnamed x38, local copies, waits for them, and re-layouts  57.7 us
    unnamed x5, waiting for transfers between devices  39.9 us
    all_to_all x6, starting transfers between devices, sent_to_all(): lax.all_to_all(jnp.broadcast_to(shard[None], (devices, *shard.shape)), ax...  35.7 us
    all_to_all x6, waiting for transfers between devices, sent_to_all(): lax.all_to_all(jnp.broadcast_to(shard[None], (devices, *shard.shape)), ax...  30.5 us
    dot_general x1, matrix products, shards(): jnp.dot(hidden_rows, lax.all_gather(down_weight, MEMBER, axis=1, tiled=Tr...  25.7 us
    convert_element_type x2, local copies, waits for them, and re-layouts, shards(): d_slices.astype(jnp.float32) * score[:, None, None, None]  23.1 us
    all_to_all x4, blocking collectives, sent_to_all(): lax.all_to_all(jnp.broadcast_to(shard[None], (devices, *shard.shape)), ax...  18.4 us
    all_to_all x1, waiting for transfers between devices, shards(): lax.all_to_all(d_sel, MEMBER, split_axis=3, concat_axis=0, tiled=True)  15 us
  transfers between devices with their start and end apart: 14, of which 9 were waited for; matrix products, arithmetic and copies ran while one was open for 34% of the time, Pallas kernels for 0%

commit v1 on v0

--- a/solution.py
+++ b/solution.py
@@ -1,3 +1,4 @@
+import functools
 import math
 import jax
 import jax.numpy as jnp
@@ -10,6 +11,17 @@
 MEMBER = ("member_0", "member_1", "member_2")
 TENSOR = ("tensor_0", "tensor_1")
 perturb_gain = 0.5
+
+
+def _track_columns(my_data, ndim_at, axis_k):
+    upper = jnp.split(my_data, lax.axis_size(MEMBER), axis=ndim_at)
+    part_now = jnp.stack(upper, axis=0)
+    return jnp.concatenate(
+        lax.all_to_all(part_now, MEMBER, concat_axis=0, split_axis=0), axis=axis_k
+    )
+
+
+tails_switch = functools.partial(_track_columns, ndim_at=3, axis_k=0)
 
 
 def sent_to_all(shard, axis):
@@ -84,7 +96,7 @@
     rank_size = d_table.shape[2]
     d_sel = jnp.take(d_table, seeds, axis=0)
     selected_factors = jnp.take(f_table, seeds, axis=0)
-    d_slices = lax.all_to_all(d_sel, MEMBER, split_axis=3, concat_axis=0, tiled=True)
+    d_slices = tails_switch(d_sel)
     f_all, fit_all = (
         gather_axes(selected_factors, (("member_0", "member_1"), "member_2"), 0),
         gather_axes(fitness.astype(jnp.bfloat16), (("member_0", "member_1"), "member_2"), 0).astype(

time: 371 us -> 326 us (0.88)
  local copies, waits for them, and re-layouts: 123 us -> 53.5 us
  waiting for transfers between devices: 98.7 us -> 128 us
    unnamed x38 -> x61, local copies, waits for them, and re-layouts: 57.7 us -> 22.1 us
    unnamed x5, waiting for transfers between devices: 39.9 us -> 66.6 us
    convert_element_type x2 -> x1, local copies, waits for them, and re-layouts: 23.1 us -> 2.03 us  [shards(): d_slices.astype(jnp.float32) * score[:, None, None, None]]
    select_n x1 -> x0, local copies, waits for them, and re-layouts: 15 us -> none  [shards(): d_sel = jnp.take(d_table, seeds, axis=0)]
  transfers between devices with their start and end apart: 14 -> 14, of which waited for: 9 -> 11; matrix products, arithmetic and copies ran while one was open for 34% -> 16% of each run, Pallas kernels for 0% -> 0%
where the time goes in v1:
time: 326 us; the launch traced here: 324 us
  waiting for transfers between devices  128 us (39%)
  starting transfers between devices  59.7 us (18%)
  local copies, waits for them, and re-layouts  53.5 us (16%)
  matrix products  39.5 us (12%)
  blocking collectives  19.2 us (6%)
  between operations  15.6 us (5%)
  other arithmetic  8.47 us (3%)
    unnamed x5, waiting for transfers between devices  66.6 us
    all_to_all x6, starting transfers between devices, sent_to_all(): lax.all_to_all(jnp.broadcast_to(shard[None], (devices, *shard.shape)), ax...  34.8 us
    all_to_all x6, waiting for transfers between devices, sent_to_all(): lax.all_to_all(jnp.broadcast_to(shard[None], (devices, *shard.shape)), ax...  30.8 us
    dot_general x1, matrix products, shards(): jnp.dot(hidden_rows, lax.all_gather(down_weight, MEMBER, axis=1, tiled=Tr...  25.7 us
    unnamed x61, local copies, waits for them, and re-layouts  22.1 us
    all_to_all x4, blocking collectives, sent_to_all(): lax.all_to_all(jnp.broadcast_to(shard[None], (devices, *shard.shape)), ax...  19.2 us
    all_to_all x1, waiting for transfers between devices, _track_columns(): lax.all_to_all(part_now, MEMBER, concat_axis=0, split_axis=0)  17.2 us
    all_to_all x2, starting transfers between devices, sum_in_two_steps(): lax.all_to_all(own.astype(jnp.bfloat16), far, 0, 0, tiled=True)  12.6 us
  transfers between devices with their start and end apart: 14, of which 11 were waited for; matrix products, arithmetic and copies ran while one was open for 16% of the time, Pallas kernels for 0%

profile of v1, /device:TPU:2, one launch (start us, length us, event | category | flops | bytes accessed | tf_op | source)
XLA Modules:
  0.0 324.1 jit_solution(8344559745957618734)
XLA Ops:
  7.2 0.7 all-gather.2.cloned.1.call-update
  7.9 1.5 convolution_convert_fusion.1
  9.7 0.7 copy.176
  10.4 3.6 %all-to-all-start.5 = ((bf16[2,8,8,864]{3,2,1,0:T(8,128)(2,1)}), bf16[2,8,8,864]{3,2,1,0:T(8,128)(2,1)S(1)}, u32[]{:S(2)}, u32[]{:S(2)}) async-start(bf16[2,8,8,864]{3,2,1,0:T(8,128)(2,1)} %copy.176), calls=%async_computation.5 | async-start | bytes 458752 | tf_op jit(solution)/shard_map/all_to_all | solution.py:63
  14.6 0.7 copy.167
  15.5 3.4 %all-to-all-start = ((bf16[2,8,8,864]{3,2,1,0:T(8,128)(2,1)}), bf16[2,8,8,864]{3,2,1,0:T(8,128)(2,1)S(1)}, u32[]{:S(2)}, u32[]{:S(2)}) async-start(bf16[2,8,8,864]{3,2,1,0:T(8,128)(2,1)} %copy.167), calls=%async_computation | async-start | bytes 458752 | tf_op jit(solution)/shard_map/all_to_all | solution.py:63
  18.9 0.7 reduce_sum.77
  19.6 0.8 all-to-all-done
  20.4 7.5 %all-to-all-start.6 = ((bf16[8,8,864]{2,1,0:T(8,128)(2,1)}), bf16[8,8,864]{2,1,0:T(8,128)(2,1)S(1)}, u32[]{:S(2)}, u32[]{:S(2)}) async-start(bf16[8,8,864]{2,1,0:T(8,128)(2,1)} %reduce_sum.77), calls=%async_computation.6 | async-start | bytes 229376 | tf_op jit(solution)/shard_map/all_to_all | solution.py:71
  27.9 0.7 reduce_sum.75
  28.6 6.3 %all-to-all-done.6 = bf16[8,8,864]{2,1,0:T(8,128)(2,1)S(1)} async-done(((bf16[8,8,864]{2,1,0:T(8,128)(2,1)}), bf16[8,8,864]{2,1,0:T(8,128)(2,1)S(1)}, u32[]{:S(2)}, u32[]{:S(2)}) %all-to-all-start.6) | async-done | bytes 110624 | tf_op jit(solution)/shard_map/all_to_all | solution.py:71
  34.9 5.2 %all-to-all-start.1 = ((bf16[8,8,864]{2,1,0:T(8,128)(2,1)}), bf16[8,8,864]{2,1,0:T(8,128)(2,1)S(1)}, u32[]{:S(2)}, u32[]{:S(2)}) async-start(bf16[8,8,864]{2,1,0:T(8,128)(2,1)} %reduce_sum.75), calls=%async_computation.1 | async-start | bytes 229376 | tf_op jit(solution)/shard_map/all_to_all | solution.py:71
  40.1 6.3 %all-to-all-done.1 = bf16[8,8,864]{2,1,0:T(8,128)(2,1)S(1)} async-done(((bf16[8,8,864]{2,1,0:T(8,128)(2,1)}), bf16[8,8,864]{2,1,0:T(8,128)(2,1)S(1)}, u32[]{:S(2)}, u32[]{:S(2)}) %all-to-all-start.1) | async-done | bytes 110624 | tf_op jit(solution)/shard_map/all_to_all | solution.py:71
  46.4 0.7 broadcast_in_dim.52
  47.1 5.1 %all-to-all-start.7 = ((bf16[8,8,864]{2,1,0:T(8,128)(2,1)}), bf16[8,8,864]{2,1,0:T(8,128)(2,1)S(1)}, u32[]{:S(2)}, u32[]{:S(2)}) async-start(bf16[8,8,864]{2,1,0:T(8,128)(2,1)} %broadcast_in_dim.52), calls=%async_computation.7 | async-start | bytes 229376 | tf_op jit(solution)/shard_map/all_to_all | solution.py:29
  52.2 6.3 %all-to-all-done.7 = bf16[8,8,864]{2,1,0:T(8,128)(2,1)S(1)} async-done(((bf16[8,8,864]{2,1,0:T(8,128)(2,1)}), bf16[8,8,864]{2,1,0:T(8,128)(2,1)S(1)}, u32[]{:S(2)}, u32[]{:S(2)}) %all-to-all-start.7) | async-done | bytes 110624 | tf_op jit(solution)/shard_map/all_to_all | solution.py:29
  58.6 4.6 %all_to_all.76 = bf16[2,8,8,864]{3,2,1,0:T(8,128)(2,1)} all-to-all(bf16[2,8,8,864]{3,2,1,0:T(8,128)(2,1)S(1)} %broadcast_in_dim.53), channel_id=1, replica_groups=mesh['member_0'=4,'member_1'=2,'member_2'=2,'tensor_0'=8,'tensor_1'=2] {..., dimensions={0} | all-to-all | bytes 442368 | tf_op jit(solution)/shard_map/all_to_all | solution.py:29
  63.2 0.7 broadcast_in_dim.44
  63.8 4.8 %all-to-all-start.2 = ((bf16[8,8,864]{2,1,0:T(8,128)(2,1)}), bf16[8,8,864]{2,1,0:T(8,128)(2,1)S(1)}, u32[]{:S(2)}, u32[]{:S(2)}) async-start(bf16[8,8,864]{2,1,0:T(8,128)(2,1)} %broadcast_in_dim.44), calls=%async_computation.2 | async-start | bytes 229376 | tf_op jit(solution)/shard_map/all_to_all | solution.py:29
  68.7 2.3 gather_fusion
  71.0 4.4 %all-to-all-done.2 = bf16[8,8,864]{2,1,0:T(8,128)(2,1)S(1)} async-done(((bf16[8,8,864]{2,1,0:T(8,128)(2,1)}), bf16[8,8,864]{2,1,0:T(8,128)(2,1)S(1)}, u32[]{:S(2)}, u32[]{:S(2)}) %all-to-all-start.2) | async-done | bytes 110624 | tf_op jit(solution)/shard_map/all_to_all | solution.py:29
  75.4 4.6 %all_to_all.77 = bf16[2,8,8,864]{3,2,1,0:T(8,128)(2,1)} all-to-all(bf16[2,8,8,864]{3,2,1,0:T(8,128)(2,1)S(1)} %broadcast_in_dim.45), channel_id=1, replica_groups=mesh['member_0'=4,'member_1'=2,'member_2'=2,'tensor_0'=8,'tensor_1'=2] {..., dimensions={0} | all-to-all | bytes 442368 | tf_op jit(solution)/shard_map/all_to_all | solution.py:29
  80.0 1.3 broadcast_in_dim.49
  81.4 5.1 %all-to-all-start.4 = ((bf16[16,128,320]{1,2,0:T(8,128)(2,1)}), bf16[16,128,320]{1,2,0:T(8,128)(2,1)S(1)}, u32[]{:S(2)}, u32[]{:S(2)}) async-start(bf16[16,128,320]{1,2,0:T(8,128)(2,1)} %broadcast_in_dim.49), calls=%async_computation.4 | async-start | bytes 2621440 | tf_op jit(solution)/shard_map/all_to_all | solution.py:29
  87.1 2.6 gather_fusion.1
  89.7 1.3 copy.172
  91.0 1.5 reshape.107
  92.5 1.1 broadcast_select_fusion
  93.7 0.8 copy.177
  94.5 2.0 copy.206
  96.4 1.0 convert_bitcast_fusion.2
  97.4 0.8 copy.168
  98.2 2.0 copy.205
  100.2 7.8 %all-to-all-done.4 = bf16[16,128,320]{1,2,0:T(8,128)(2,1)S(1)} async-done(((bf16[16,128,320]{1,2,0:T(8,128)(2,1)}), bf16[16,128,320]{1,2,0:T(8,128)(2,1)S(1)}, u32[]{:S(2)}, u32[]{:S(2)}) %all-to-all-start.4) | async-done | bytes 1310752 | tf_op jit(solution)/shard_map/all_to_all | solution.py:29
  108.4 1.2 fusion.18
  109.9 3.9 %copy.181 = f32[8,1,128,864]{2,0,3,1:T(8,128)} copy(f32[8,1,128,864]{2,3,1,0:T(8,128)S(1)} %slice_multiply_fusion) | data formatting | bytes 7077888 | tf_op jit(solution)/shard_map/mul | solution.py:125
  114.1 3.9 %copy.174 = f32[8,1,128,864]{2,0,3,1:T(8,128)} copy(f32[8,1,128,864]{2,3,0,1:T(8,128)S(1)} %fusion.2) | data formatting | bytes 7077888 | tf_op jit(solution)/shard_map/mul | solution.py:124
  117.9 2.0 add.60.clone
  119.9 2.0 add.55.clone
  122.0 25.7 %convolution_convert_fusion = bf16[1024,5120]{1,0:T(8,128)(2,1)} fusion(bf16[864,5120]{0,1:T(8,128)(2,1)} %all-gather.2.cloned.1.call-done, f32[108,8,8,128]{3,2,1,0:T(8,128)} %bitcast.218, f32[108,8,8,128]{3,2,1,0:T(8,128)} %bitcast.220, f32[108,8,8,128]{3,2,1,0:T(8,128)} %bitcast.219, f32[108,8,8,128]{3,2,1,0:T(8,128)} %bitcast.221), kind=kOutput, calls=%fused_computation.2 | convolution fusion | flops 9072017408 | bytes 33488896 | tf_op jit(solution)/shard_map/dot_general | solution.py:132
  147.6 14.4 %copy.196 = bf16[1024,5120]{0,1:T(8,128)(2,1)} copy(bf16[1024,5120]{1,0:T(8,128)(2,1)} %convolution_convert_fusion) | data formatting | bytes 20971520
  162.1 0.6 copy-done.18
  163.3 8.5 %all-to-all-start.11 = ((bf16[8,1,8]{2,1,0:T(2,128)(2,1)}), bf16[8,1,8]{2,1,0:T(2,128)(2,1)S(1)}, u32[]{:S(2)}, u32[]{:S(2)}) async-start(bf16[8,1,8]{2,1,0:T(2,128)(2,1)} %broadcast_in_dim.98), calls=%async_computation.11 | async-start | bytes 8192 | tf_op jit(solution)/shard_map/all_to_all | solution.py:29
  172.8 5.2 %all-to-all-done.11 = bf16[8,1,8]{2,1,0:T(2,128)(2,1)S(1)} async-done(((bf16[8,1,8]{2,1,0:T(2,128)(2,1)}), bf16[8,1,8]{2,1,0:T(2,128)(2,1)S(1)}, u32[]{:S(2)}, u32[]{:S(2)}) %all-to-all-start.11) | async-done | bytes 160 | tf_op jit(solution)/shard_map/all_to_all | solution.py:29
  178.0 3.7 %all_to_all.78 = bf16[2,8,8]{2,1,0:T(8,128)(2,1)S(1)} all-to-all(bf16[2,8,8]{2,1,0:T(8,128)(2,1)S(1)} %broadcast_in_dim.100), channel_id=1, replica_groups=mesh['member_0'=4,'member_1'=2,'member_2'=2,'tensor_0'=8,'tensor_1'=2] {..., dimensions={0} | all-to-all | bytes 512 | tf_op jit(solution)/shard_map/all_to_all | solution.py:29
  181.7 5.0 %all-to-all-start.10 = ((bf16[16,8,3,4,320]{4,1,3,2,0:T(8,128)(2,1)}), bf16[16,8,3,4,320]{4,1,3,2,0:T(8,128)(2,1)S(1)}, u32[]{:S(2)}, u32[]{:S(2)}) async-start(bf16[16,8,3,4,320]{4,1,3,2,0:T(8,128)(2,1)} %copy-done.12), calls=%async_computation.10 | async-start | bytes 2359296 | tf_op jit(solution)/shard_map/all_to_all | solution.py:20
  186.7 17.2 %all-to-all-done.10 = bf16[16,8,3,4,320]{4,1,3,2,0:T(8,128)(2,1)S(1)} async-done(((bf16[16,8,3,4,320]{4,1,3,2,0:T(8,128)(2,1)}), bf16[16,8,3,4,320]{4,1,3,2,0:T(8,128)(2,1)S(1)}, u32[]{:S(2)}, u32[]{:S(2)}) %all-to-all-start.10) | async-done | bytes 983072 | tf_op jit(solution)/shard_map/all_to_all | solution.py:20
  203.9 1.3 broadcast_in_dim.101
  205.4 5.8 %all-to-all-start.13 = ((bf16[8,8,3,4,864]{4,1,3,2,0:T(8,128)(2,1)}), bf16[8,8,3,4,864]{4,1,3,2,0:T(8,128)(2,1)S(1)}, u32[]{:S(2)}, u32[]{:S(2)}) async-start(bf16[8,8,3,4,864]{4,1,3,2,0:T(8,128)(2,1)} %broadcast_in_dim.101), calls=%async_computation.13 | async-start | bytes 2752512 | tf_op jit(solution)/shard_map/all_to_all | solution.py:29
  212.5 0.6 fusion.39
  213.8 65.9 %reduce-scatter.7.cloned.1.call-done = bf16[640,1024]{1,0:T(8,128)(2,1)} async-done(((bf16[5120,1024]{1,0:T(8,128)(2,1)}), bf16[640,1024]{1,0:T(8,128)(2,1)}) %reduce-scatter.7.cloned.1.call-update) | async-done | bytes 1310736
  279.8 1.6 copy_bitcast_fusion
  281.5 2.0 copy.189
  283.5 1.2 multiply_convert_fusion
  285.3 6.2 %all_to_all.79 = bf16[2,8,8,3,4,864]{5,2,1,4,3,0:T(8,128)(2,1)S(1)} all-to-all(bf16[2,8,8,3,4,864]{5,2,1,4,3,0:T(8,128)(2,1)S(1)} %broadcast_in_dim.102), channel_id=1, replica_groups=mesh['member_0'=4,'member_1'=2,'member_2'=2,'tensor_0'=8,'tensor_1'=2] {..., dimensions={0} | all-to-all | bytes 5308416 | tf_op jit(solution)/shard_map/all_to_all | solution.py:29
  291.8 1.5 copy-done.13
  293.2 1.3 fusion.16
  295.2 1.5 fusion.7
  296.7 0.7 broadcast_in_dim.54
  297.4 5.5 %all-to-all-start.9 = ((f32[16,8,128,4]{2,1,3,0:T(8,128)}), f32[16,8,128,4]{2,1,3,0:T(8,128)S(1)}, u32[]{:S(2)}, u32[]{:S(2)}) async-start(f32[16,8,128,4]{2,1,3,0:T(8,128)} %broadcast_in_dim.54), calls=%async_computation.9 | async-start | bytes 524288 | tf_op jit(solution)/shard_map/all_to_all | solution.py:29
  302.9 2.6 fusion.15
  305.5 2.5 fusion.14
  308.0 7.1 %all-to-all-done.9 = f32[16,8,128,4]{2,1,3,0:T(8,128)S(1)} async-done(((f32[16,8,128,4]{2,1,3,0:T(8,128)}), f32[16,8,128,4]{2,1,3,0:T(8,128)S(1)}, u32[]{:S(2)}, u32[]{:S(2)}) %all-to-all-start.9) | async-done | bytes 262176 | tf_op jit(solution)/shard_map/all_to_all | solution.py:29
  315.2 2.3 fusion.13
  (100 shorter events, 6.7 us)
Async XLA Ops:
  7.2 61.5 %copy-start = (bf16[16,3,4,5120]{3,2,1,0:T(4,128)(2,1)S(1)}, bf16[16,3,4,5120]{3,2,1,0:T(4,128)(2,1)}, u32[]{:S(2)}) copy-start(bf16[16,3,4,5120]{3,2,1,0:T(4,128)(2,1)} %param.12) | copy-start | bytes 5898244
  7.2 6.8 %copy-start.15 = (bf16[128,320]{0,1:T(8,128)(2,1)S(1)}, bf16[128,320]{0,1:T(8,128)(2,1)}, u32[]{:S(2)}) copy-start(bf16[128,320]{0,1:T(8,128)(2,1)} %param.8) | copy-start | bytes 245764
  7.2 6.8 %copy-start.16 = (bf16[320,864]{1,0:T(8,128)(2,1)S(1)}, bf16[320,864]{1,0:T(8,128)(2,1)}, u32[]{:S(2)}) copy-start(bf16[320,864]{1,0:T(8,128)(2,1)} %param.9) | copy-start | bytes 1658884
  7.2 110.7 %all-gather.2.cloned.1.call-start = ((), (), s32[]{:S(2)}) async-start(), calls=%async_computation.17 | async-start | bytes 9748480 | tf_op jit(solution)/shard_map/all_gather | solution.py:134
  10.4 29.7 %copy-start.17 = (s32[8]{0:T(128)S(1)}, s32[8]{0:T(128)}, u32[]{:S(2)}) copy-start(s32[8]{0:T(128)} %param.14) | copy-start | bytes 100
  10.4 5.1 %all-to-all-start.5 = ((bf16[2,8,8,864]{3,2,1,0:T(8,128)(2,1)}), bf16[2,8,8,864]{3,2,1,0:T(8,128)(2,1)S(1)}, u32[]{:S(2)}, u32[]{:S(2)}) async-start(bf16[2,8,8,864]{3,2,1,0:T(8,128)(2,1)} %copy.176), calls=%async_computation.5 | async-start | bytes 458752 | tf_op jit(solution)/shard_map/all_to_all | solution.py:63
  15.5 5.0 %all-to-all-start = ((bf16[2,8,8,864]{3,2,1,0:T(8,128)(2,1)}), bf16[2,8,8,864]{3,2,1,0:T(8,128)(2,1)S(1)}, u32[]{:S(2)}, u32[]{:S(2)}) async-start(bf16[2,8,8,864]{3,2,1,0:T(8,128)(2,1)} %copy.167), calls=%async_computation | async-start | bytes 458752 | tf_op jit(solution)/shard_map/all_to_all | solution.py:63
  20.4 14.4 %all-to-all-start.6 = ((bf16[8,8,864]{2,1,0:T(8,128)(2,1)}), bf16[8,8,864]{2,1,0:T(8,128)(2,1)S(1)}, u32[]{:S(2)}, u32[]{:S(2)}) async-start(bf16[8,8,864]{2,1,0:T(8,128)(2,1)} %reduce_sum.77), calls=%async_computation.6 | async-start | bytes 229376 | tf_op jit(solution)/shard_map/all_to_all | solution.py:71
  34.9 11.6 %all-to-all-start.1 = ((bf16[8,8,864]{2,1,0:T(8,128)(2,1)}), bf16[8,8,864]{2,1,0:T(8,128)(2,1)S(1)}, u32[]{:S(2)}, u32[]{:S(2)}) async-start(bf16[8,8,864]{2,1,0:T(8,128)(2,1)} %reduce_sum.75), calls=%async_computation.1 | async-start | bytes 229376 | tf_op jit(solution)/shard_map/all_to_all | solution.py:71
  47.1 11.5 %all-to-all-start.7 = ((bf16[8,8,864]{2,1,0:T(8,128)(2,1)}), bf16[8,8,864]{2,1,0:T(8,128)(2,1)S(1)}, u32[]{:S(2)}, u32[]{:S(2)}) async-start(bf16[8,8,864]{2,1,0:T(8,128)(2,1)} %broadcast_in_dim.52), calls=%async_computation.7 | async-start | bytes 229376 | tf_op jit(solution)/shard_map/all_to_all | solution.py:29
  63.8 11.5 %all-to-all-start.2 = ((bf16[8,8,864]{2,1,0:T(8,128)(2,1)}), bf16[8,8,864]{2,1,0:T(8,128)(2,1)S(1)}, u32[]{:S(2)}, u32[]{:S(2)}) async-start(bf16[8,8,864]{2,1,0:T(8,128)(2,1)} %broadcast_in_dim.44), calls=%async_computation.2 | async-start | bytes 229376 | tf_op jit(solution)/shard_map/all_to_all | solution.py:29
  80.0 6.7 %copy-start.6 = (bf16[8,3,4,5120]{3,2,1,0:T(4,128)(2,1)S(1)}, bf16[8,3,4,5120]{3,2,1,0:T(4,128)(2,1)}, u32[]{:S(2)}) copy-start(bf16[8,3,4,5120]{3,2,1,0:T(4,128)(2,1)} %gather_fusion) | copy-start | bytes 2949124
  81.4 26.7 %all-to-all-start.4 = ((bf16[16,128,320]{1,2,0:T(8,128)(2,1)}), bf16[16,128,320]{1,2,0:T(8,128)(2,1)S(1)}, u32[]{:S(2)}, u32[]{:S(2)}) async-start(bf16[16,128,320]{1,2,0:T(8,128)(2,1)} %broadcast_in_dim.49), calls=%async_computation.4 | async-start | bytes 2621440 | tf_op jit(solution)/shard_map/all_to_all | solution.py:29
  86.5 193.2 %reduce-scatter.7.cloned.1.call-start = ((), (), s32[]{:S(2)}) async-start(), calls=%async_computation.18 | async-start | bytes 11796480
  87.1 99.6 %copy-start.3 = (bf16[8,3,4,5120]{3,0,2,1:T(8,128)(2,1)}, bf16[8,3,4,5120]{3,0,2,1:T(8,128)(2,1)S(1)}, u32[]{:S(2)}) copy-start(bf16[8,3,4,5120]{3,0,2,1:T(8,128)(2,1)S(1)} %copy_select_fusion) | copy-start | bytes 2949124
  89.6 4.0 %copy-start.14 = (bf16[2,8,8,864]{3,2,1,0:T(8,128)(2,1)S(1)}, bf16[2,8,8,864]{3,2,1,0:T(8,128)(2,1)}, u32[]{:S(2)}) copy-start(bf16[2,8,8,864]{3,2,1,0:T(8,128)(2,1)} %all_to_all.76) | copy-start | bytes 663556
  109.6 4.2 %copy-start.2 = (f32[8,2,128,864]{2,3,1,0:T(8,128)}, f32[8,2,128,864]{2,3,1,0:T(8,128)S(1)}, u32[]{:S(2)}) copy-start(f32[8,2,128,864]{2,3,1,0:T(8,128)S(1)} %fusion.18) | copy-start | bytes 21233668
  114.1 3.9 %copy-start.8 = (f32[128,864]{0,1:T(8,128)S(1)}, f32[128,864]{0,1:T(8,128)}, u32[]{:S(2)}) copy-start(f32[128,864]{0,1:T(8,128)} %copy.206) | copy-start | bytes 1327108
  117.9 2.0 copy-start.10
  162.0 0.7 copy-start.18
  163.3 14.7 %all-to-all-start.11 = ((bf16[8,1,8]{2,1,0:T(2,128)(2,1)}), bf16[8,1,8]{2,1,0:T(2,128)(2,1)S(1)}, u32[]{:S(2)}, u32[]{:S(2)}) async-start(bf16[8,1,8]{2,1,0:T(2,128)(2,1)} %broadcast_in_dim.98), calls=%async_computation.11 | async-start | bytes 8192 | tf_op jit(solution)/shard_map/all_to_all | solution.py:29
  172.8 5.2 %copy-start.12 = (bf16[16,8,3,4,320]{4,1,3,2,0:T(8,128)(2,1)}, bf16[16,8,3,4,320]{4,1,3,2,0:T(8,128)(2,1)S(1)}, u32[]{:S(2)}) copy-start(bf16[16,8,3,4,320]{4,1,3,2,0:T(8,128)(2,1)S(1)} %fusion.20) | copy-start | bytes 2949124
  181.7 22.3 %all-to-all-start.10 = ((bf16[16,8,3,4,320]{4,1,3,2,0:T(8,128)(2,1)}), bf16[16,8,3,4,320]{4,1,3,2,0:T(8,128)(2,1)S(1)}, u32[]{:S(2)}, u32[]{:S(2)}) async-start(bf16[16,8,3,4,320]{4,1,3,2,0:T(8,128)(2,1)} %copy-done.12), calls=%async_computation.10 | async-start | bytes 2359296 | tf_op jit(solution)/shard_map/all_to_all | solution.py:20
  186.7 24.4 %slice-start.2 = ((bf16[8,3,4,5120]{3,0,2,1:T(8,128)(2,1)}), bf16[8,1,4,5120]{3,0,2,1:T(8,128)(2,1)S(1)}, s32[]{:S(2)}) async-start(bf16[8,3,4,5120]{3,0,2,1:T(8,128)(2,1)} %copy-done.3), calls=%async_computation.22 | async-start | bytes 655360 | tf_op jit(solution)/shard_map/slice | solution.py:140
  203.9 1.4 copy-start.4
  205.4 79.3 %all-to-all-start.13 = ((bf16[8,8,3,4,864]{4,1,3,2,0:T(8,128)(2,1)}), bf16[8,8,3,4,864]{4,1,3,2,0:T(8,128)(2,1)S(1)}, u32[]{:S(2)}, u32[]{:S(2)}) async-start(bf16[8,8,3,4,864]{4,1,3,2,0:T(8,128)(2,1)} %broadcast_in_dim.101), calls=%async_computation.13 | async-start | bytes 2752512 | tf_op jit(solution)/shard_map/all_to_all | solution.py:29
  211.1 68.7 %copy-start.5 = (bf16[16,8,3,4,320]{4,1,3,2,0:T(8,128)(2,1)S(1)}, bf16[16,8,3,4,320]{4,1,3,2,0:T(8,128)(2,1)}, u32[]{:S(2)}) copy-start(bf16[16,8,3,4,320]{4,1,3,2,0:T(8,128)(2,1)} %copy-done.4) | copy-start | bytes 2949124
  211.1 104.1 %reduce-scatter.9.cloned.1.call-start = ((), (), s32[]{:S(2)}) async-start(), calls=%async_computation.19 | async-start | bytes 1966080
  285.3 9.3 %slice-start = ((s8[7077888]{0:T(1024)(128)(4,1)}), s8[4194304]{0:T(1024)(128)(4,1)S(1)}, s32[]{:S(2)}) async-start(s8[7077888]{0:T(1024)(128)(4,1)} %bitcast.214), calls=%async_computation.20 | async-start | bytes 8388608
  291.5 1.7 copy-start.13
  291.5 3.4 %slice-start.1 = ((s8[7077888]{0:T(1024)(128)(4,1)}), s8[2883584]{0:T(1024)(128)(4,1)S(1)}, s32[]{:S(2)}) async-start(s8[7077888]{0:T(1024)(128)(4,1)} %bitcast.214), calls=%async_computation.21 | async-start | bytes 5767168
  291.8 4.9 %copy-start.7 = (bf16[8,2,8,3,4,864]{5,2,1,0,4,3:T(8,128)(2,1)}, bf16[8,2,8,3,4,864]{5,2,1,0,4,3:T(8,128)(2,1)S(1)}, u32[]{:S(2)}) copy-start(bf16[8,2,8,3,4,864]{5,2,1,0,4,3:T(8,128)(2,1)S(1)} %copy.192) | copy-start | bytes 7962628
  291.8 3.3 %copy-start.9 = (f32[128,864]{0,1:T(8,128)S(1)}, f32[128,864]{0,1:T(8,128)}, u32[]{:S(2)}) copy-start(f32[128,864]{0,1:T(8,128)} %copy.206) | copy-start | bytes 1327108
  291.8 3.4 %copy-start.11 = (f32[128,864]{0,1:T(8,128)S(1)}, f32[128,864]{0,1:T(8,128)}, u32[]{:S(2)}) copy-start(f32[128,864]{0,1:T(8,128)} %copy.205) | copy-start | bytes 1327108
  297.4 17.7 %all-to-all-start.9 = ((f32[16,8,128,4]{2,1,3,0:T(8,128)}), f32[16,8,128,4]{2,1,3,0:T(8,128)S(1)}, u32[]{:S(2)}, u32[]{:S(2)}) async-start(f32[16,8,128,4]{2,1,3,0:T(8,128)} %broadcast_in_dim.54), calls=%async_computation.9 | async-start | bytes 524288 | tf_op jit(solution)/shard_map/all_to_all | solution.py:29
  302.9 14.7 %copy-start.1 = (bf16[16,3,4,5120]{3,2,1,0:T(4,128)(2,1)S(1)}, bf16[16,3,4,5120]{3,2,1,0:T(4,128)(2,1)}, u32[]{:S(2)}) copy-start(bf16[16,3,4,5120]{3,2,1,0:T(4,128)(2,1)} %param.12) | copy-start | bytes 5898244
Sparse Core Ops, SparseCore 0:
  10.7 97.9 all-gather.1
  162.2 117.4 reduce-scatter.6
  282.2 27.6 reduce-scatter.8
